TPU v7x, 32 devices: a whole 2x2x4 slice. The times are simulated.
32 devices in a mesh: blk: 8 (over y, x, core), sub: 4 (over z).
Axes of the slice: x: 2, y: 2, z: 4, core: 2. Of those that a mesh axis runs over, the one named last changes fastest.
Arguments:
- flow_state: float32 [6, 64, 8, 512], P(None, 'blk', None, 'sub'), may hold values from -6 to 6
- timestep: float32 [64, 8, 512], P('blk', None, 'sub'), may hold values from 0.05 to 0.3
- coupling: float32 [3, 6, 6], replicated, may hold values from -2.5 to 2.5
- face_type: int32 [8, 2], P('blk'), may hold values from 0 to 3
- face_rot: int32 [8, 2], P('blk'), may hold values from 0 to 3
Outputs:
- updated: float32 [6, 64, 8, 512], P(None, 'blk', None, 'sub')
- fine_residual: float32 [6, 64, 8, 512], P(None, 'blk', None, 'sub')
All inputs are finite; a program needn't handle non-finite values.
Results may differ from a plain program's by a relative error of at most 0.0003.
Values sent between devices are 32-bit elements; how exact they have to be, the bound alone decides.
A program may use at most 64 MiB of HBM per device.

v0:
```python
import jax
import jax.numpy as jnp
from jax import lax
from jax.sharding import PartitionSpec as P

DAMP_TWO = 0.05
DAMP_FOUR = 0.02
SECTION_COEFFS = (0.4, 1.0)
PRECISE = lax.Precision.HIGHEST


def extended(cells, sides, width):
    for axis, dim in sides:
        count = lax.axis_size(axis)
        head = lax.slice_in_dim(cells, 0, width, axis=dim)
        tail = lax.slice_in_dim(cells, cells.shape[dim] - width, cells.shape[dim], axis=dim)
        cells = jnp.concatenate(
            [
                lax.ppermute(tail, axis, [(i, (i + 1) % count) for i in range(count)]),
                cells,
                lax.ppermute(head, axis, [((i + 1) % count, i) for i in range(count)]),
            ],
            axis=dim,
        )
    return cells


def rotate_plane(plane, rot_code):
    flipped = jnp.where(rot_code % 2 == 1, plane[:, :, ::-1, :], plane)
    turned = jnp.stack([flipped[0], flipped[1], -flipped[3], flipped[2], flipped[4], flipped[5]])
    return jnp.where(rot_code // 2 % 2 == 1, turned, flipped)


def mirrored(rows_in, negated):
    sign_row = jnp.where(jnp.arange(6) == negated, -1.0, 1.0).astype(jnp.float32)
    return rows_in * sign_row[:, None, None, None]


def lower_ghosts(block_cells, prev_last, next_first, kind_code, rot_code):
    wall_rows = mirrored(block_cells[:, :2][:, ::-1], 1)
    picked = jnp.where(
        kind_code == 0,
        prev_last,
        jnp.where(
            kind_code == 1,
            next_first[:, ::-1],
            jnp.where(kind_code == 2, wall_rows, jnp.zeros_like(wall_rows)),
        ),
    )
    return rotate_plane(picked, rot_code)


def upper_ghosts(block_cells, prev_last, next_first, kind_code, rot_code):
    wall_rows = mirrored(block_cells[:, -2:][:, ::-1], 1)
    picked = jnp.where(
        kind_code == 0,
        next_first,
        jnp.where(
            kind_code == 1,
            prev_last[:, ::-1],
            jnp.where(kind_code == 2, wall_rows, jnp.zeros_like(wall_rows)),
        ),
    )
    return rotate_plane(picked, rot_code)


def flux_of(padded, coupling, direction):
    mixed = jnp.einsum("uv,vijk->uijk", coupling[direction], padded, precision=PRECISE)
    return mixed + 0.5 * padded[1 + direction][None] * padded


def divergence(padded, coupling, direction):
    axis_pos = direction + 1
    length = padded.shape[axis_pos] - 4
    fluxes = flux_of(padded, coupling, direction)
    face_count = length + 1

    def cut_axis(array, offset, amount):
        return lax.slice_in_dim(array, offset, offset + amount, axis=axis_pos)

    near_left = cut_axis(padded, 1, face_count)
    near_right = cut_axis(padded, 2, face_count)
    far_left = cut_axis(padded, 0, face_count)
    far_right = cut_axis(padded, 3, face_count)
    face_flux = (
        0.5 * (cut_axis(fluxes, 1, face_count) + cut_axis(fluxes, 2, face_count))
        - DAMP_TWO * (near_right - near_left)
        + DAMP_FOUR * (far_right - 3.0 * near_right + 3.0 * near_left - far_left)
    )
    return cut_axis(face_flux, 1, length) - cut_axis(face_flux, 0, length)


def cell_residual(along_i, along_k, block_cells, coupling):
    low_j = mirrored(block_cells[:, :, :2][:, :, ::-1], 2)
    high_j = mirrored(block_cells[:, :, -2:][:, :, ::-1], 2)
    along_j = jnp.concatenate([low_j, block_cells, high_j], axis=2)
    return (
        divergence(along_i, coupling, 0)
        + divergence(along_j, coupling, 1)
        + divergence(along_k, coupling, 2)
    )


def from_halo(raw_i, along_k, block_cells, coupling, face_type, face_rot):
    prev_last = raw_i[:, :2]
    next_first = raw_i[:, -2:]
    low_ghost = lower_ghosts(block_cells, prev_last, next_first, face_type[0, 0], face_rot[0, 0])
    high_ghost = upper_ghosts(block_cells, prev_last, next_first, face_type[0, 1], face_rot[0, 1])
    along_i = jnp.concatenate([low_ghost, block_cells, high_ghost], axis=1)
    return cell_residual(along_i, along_k, block_cells, coupling)


def clear_ends(padded, width):
    final_index = lax.axis_size("sub") - 1
    position = lax.axis_index("sub")
    columns = jnp.arange(padded.shape[3])
    outside = (columns < width) & (position == 0) | (columns >= padded.shape[3] - width) & (
        position == final_index
    )
    return jnp.where(outside[None, None, None, :], 0.0, padded)


def restrict(array):
    shape_of = array.shape
    leading = shape_of[:-3]
    reshaped = array.reshape(
        leading + (shape_of[-3] // 2, 2, shape_of[-2] // 2, 2, shape_of[-1] // 2, 2)
    )
    return reshaped.mean(axis=(-5, -3, -1))


def prolong(array):
    return jnp.repeat(jnp.repeat(jnp.repeat(array, 2, axis=-3), 2, axis=-2), 2, axis=-1)


def body(flow_state, timestep, coupling, face_type, face_rot):
    fine_state = flow_state
    for section_alpha in SECTION_COEFFS:
        fine_padded = extended(fine_state, (("blk", 1), ("sub", 3)), 2)
        fine_padded = clear_ends(fine_padded, 2)
        fine_state = flow_state - section_alpha * timestep[None] * from_halo(
            fine_padded[:, :, :, 2:-2],
            fine_padded[:, 2:-2],
            fine_state,
            coupling,
            face_type,
            face_rot,
        )
    coarse_start = restrict(fine_state)
    coarse_step = restrict(timestep)
    padded = extended(fine_state, (("blk", 1), ("sub", 3)), 2)
    padded = clear_ends(padded, 2)
    residual_now = from_halo(
        padded[:, :, :, 2:-2], padded[:, 2:-2], fine_state, coupling, face_type, face_rot
    )
    coarse_pad = extended(coarse_start, (("blk", 1), ("sub", 3)), 2)
    coarse_pad = clear_ends(coarse_pad, 2)
    start_residual = from_halo(
        coarse_pad[:, :, :, 2:-2], coarse_pad[:, 2:-2], coarse_start, coupling, face_type, face_rot
    )
    forcing = start_residual - restrict(residual_now)
    coarse = coarse_start
    for section_alpha in SECTION_COEFFS:
        coarse_padded = extended(coarse, (("blk", 1), ("sub", 3)), 2)
        coarse_padded = clear_ends(coarse_padded, 2)
        coarse = coarse_start - section_alpha * coarse_step[None] * (
            from_halo(
                coarse_padded[:, :, :, 2:-2],
                coarse_padded[:, 2:-2],
                coarse,
                coupling,
                face_type,
                face_rot,
            )
            - forcing
        )
    updated = fine_state + prolong(coarse - coarse_start)
    return (updated, residual_now)


def solution(mesh):
    return jax.shard_map(
        body,
        mesh=mesh,
        in_specs=(
            P(None, "blk", None, "sub"),
            P("blk", None, "sub"),
            P(),
            P("blk", None),
            P("blk", None),
        ),
        out_specs=(P(None, "blk", None, "sub"), P(None, "blk", None, "sub")),
        check_vma=False,
    )
```

profile of v0, /device:TPU:0, one launch (start us, length us, event | category | flops | bytes accessed | tf_op | source)
XLA Modules:
  0.0 146.8 jit_solution(11204201667991587793)
XLA Ops:
  0.6 1.0 copy.127
  2.2 2.9 %collective-permute-start.1 = (f32[6,2,8,128]{3,1,2,0:T(2,128)S(1)}, f32[6,2,8,128]{3,1,2,0:T(2,128)S(1)}, u32[]{:S(2)}, u32[]{:S(2)}) collective-permute-start(f32[6,2,8,128]{3,1,2,0:T(2,128)S(1)} %get-tuple-element.43), channel_id=1, source_target_pairs={{4,0},{8,4},{12,8},{16,12},{20,16},{24,20},{28,24},{0,28},{5,1},{9... | collective-permute-start | bytes 147464 | tf_op jit(solution)/shard_map/ppermute | solution.py:21
  5.1 0.8 broadcast_multiply_fusion.1
  5.9 2.8 %reshape.73 = f32[4,2,4,2,64,2]{5,4,3,2,1,0:T(8,128)S(1)} reshape(f32[8,8,128]{2,1,0:T(8,128)} %param.6) | data formatting | bytes 65536 | tf_op jit(solution)/shard_map/reshape | solution.py:126
  8.8 1.3 fusion.232
  10.1 1.4 fusion.231
  11.6 0.6 fusion.62
  13.1 2.3 %collective-permute-start.2 = (f32[6,12,8,2]{3,1,2,0:T(8,128)S(1)}, f32[6,12,8,2]{3,1,2,0:T(8,128)S(1)}, u32[]{:S(2)}, u32[]{:S(2)}) collective-permute-start(f32[6,12,8,2]{3,1,2,0:T(8,128)S(1)} %get-tuple-element.30), channel_id=1, source_target_pairs={{0,1},{1,2},{2,3},{3,0},{4,5},{5,6},{6,7},{7,4},{8,9},{9,10},{10,1... | collective-permute-start | bytes 13832 | tf_op jit(solution)/shard_map/ppermute | solution.py:19
  15.4 2.1 %collective-permute-start.3 = (f32[6,12,8,2]{3,1,2,0:T(8,128)S(1)}, f32[6,12,8,2]{3,1,2,0:T(8,128)S(1)}, u32[]{:S(2)}, u32[]{:S(2)}) collective-permute-start(f32[6,12,8,2]{3,1,2,0:T(8,128)S(1)} %get-tuple-element.31), channel_id=1, source_target_pairs={{1,0},{2,1},{3,2},{0,3},{5,4},{6,5},{7,6},{4,7},{9,8},{10,9},{11,1... | collective-permute-start | bytes 13832 | tf_op jit(solution)/shard_map/ppermute | solution.py:21
  26.8 0.6 collective-permute-done.2
  27.4 6.1 %collective-permute-done.3 = f32[6,12,8,2]{3,1,2,0:T(8,128)S(1)} collective-permute-done((f32[6,12,8,2]{3,1,2,0:T(8,128)S(1)}, f32[6,12,8,2]{3,1,2,0:T(8,128)S(1)}, u32[]{:S(2)}, u32[]{:S(2)}) %collective-permute-start.3) | collective-permute-done | bytes 4640 | tf_op jit(solution)/shard_map/ppermute | solution.py:21
  35.0 0.6 fusion.64
  36.3 0.8 fusion.10
  39.0 2.6 %collective-permute-start.5 = (f32[6,2,8,128]{3,1,2,0:T(2,128)S(1)}, f32[6,2,8,128]{3,1,2,0:T(2,128)S(1)}, u32[]{:S(2)}, u32[]{:S(2)}) collective-permute-start(f32[6,2,8,128]{3,1,2,0:T(2,128)S(1)} %get-tuple-element.39), channel_id=1, source_target_pairs={{4,0},{8,4},{12,8},{16,12},{20,16},{24,20},{28,24},{0,28},{5,1},{9... | collective-permute-start | bytes 147464 | tf_op jit(solution)/shard_map/ppermute | solution.py:21
  41.9 1.6 %collective-permute-done.4 = f32[6,2,8,128]{3,1,2,0:T(2,128)S(1)} collective-permute-done((f32[6,2,8,128]{3,1,2,0:T(2,128)S(1)}, f32[6,2,8,128]{3,1,2,0:T(2,128)S(1)}, u32[]{:S(2)}, u32[]{:S(2)}) %collective-permute-start.4) | collective-permute-done | bytes 49184 | tf_op jit(solution)/shard_map/ppermute | solution.py:19
  43.7 1.2 collective-permute-start.6
  44.9 2.7 %collective-permute-start.7 = (f32[6,12,8,2]{3,1,2,0:T(8,128)S(1)}, f32[6,12,8,2]{3,1,2,0:T(8,128)S(1)}, u32[]{:S(2)}, u32[]{:S(2)}) collective-permute-start(f32[6,12,8,2]{3,1,2,0:T(8,128)S(1)} %get-tuple-element.29), channel_id=1, source_target_pairs={{1,0},{2,1},{3,2},{0,3},{5,4},{6,5},{7,6},{4,7},{9,8},{10,9},{11,1... | collective-permute-start | bytes 13832 | tf_op jit(solution)/shard_map/ppermute | solution.py:21
  47.9 9.7 %collective-permute-done.6 = f32[6,12,8,2]{3,1,2,0:T(8,128)S(1)} collective-permute-done((f32[6,12,8,2]{3,1,2,0:T(8,128)S(1)}, f32[6,12,8,2]{3,1,2,0:T(8,128)S(1)}, u32[]{:S(2)}, u32[]{:S(2)}) %collective-permute-start.6) | collective-permute-done | bytes 4640 | tf_op jit(solution)/shard_map/ppermute | solution.py:19
  57.6 7.2 %collective-permute-done.7 = f32[6,12,8,2]{3,1,2,0:T(8,128)S(1)} collective-permute-done((f32[6,12,8,2]{3,1,2,0:T(8,128)S(1)}, f32[6,12,8,2]{3,1,2,0:T(8,128)S(1)}, u32[]{:S(2)}, u32[]{:S(2)}) %collective-permute-start.7) | collective-permute-done | bytes 4640 | tf_op jit(solution)/shard_map/ppermute | solution.py:21
  66.3 0.6 fusion.60
  67.6 0.8 fusion.8
  70.2 2.7 %copy.128 = f32[6,8,8,128]{0,3,2,1:T(8,128)} copy(f32[6,8,8,128]{3,1,2,0:T(8,128)S(1)} %fusion.97) | data formatting | bytes 393216 | tf_op jit(solution)/shard_map/sub | solution.py:141
  73.0 4.8 %reduce_sum.27 = f32[6,4,4,64]{0,3,2,1:T(8,128)S(1)} reduce(f32[6,4,2,4,2,64,2]{0,6,5,4,3,2,1:T(2,128)} %bitcast.127, f32[]{:T(128)} %constant.168.clone.1), dimensions={2,4,6}, to_apply=%region_0.1 | reduce | flops 43008 | bytes 221188 | tf_op jit(solution)/shard_map/reduce_sum | solution.py:129
  78.1 2.6 %collective-permute-start.13 = (f32[6,2,8,128]{3,1,2,0:T(2,128)S(1)}, f32[6,2,8,128]{3,1,2,0:T(2,128)S(1)}, u32[]{:S(2)}, u32[]{:S(2)}) collective-permute-start(f32[6,2,8,128]{3,1,2,0:T(2,128)S(1)} %get-tuple-element.35), channel_id=1, source_target_pairs={{4,0},{8,4},{12,8},{16,12},{20,16},{24,20},{28,24},{0,28},{5,1},{9... | collective-permute-start | bytes 147464 | tf_op jit(solution)/shard_map/ppermute | solution.py:21
  81.1 2.6 %collective-permute-start.9 = (f32[6,2,4,64]{3,0,2,1:T(8,128)S(1)}, f32[6,2,4,64]{3,0,2,1:T(8,128)S(1)}, u32[]{:S(2)}, u32[]{:S(2)}) collective-permute-start(f32[6,2,4,64]{3,0,2,1:T(8,128)S(1)} %get-tuple-element.63), channel_id=1, source_target_pairs={{4,0},{8,4},{12,8},{16,12},{20,16},{24,20},{28,24},{0,28},{5,1},{9... | collective-permute-start | bytes 36872 | tf_op jit(solution)/shard_map/ppermute | solution.py:21
  84.1 1.2 collective-permute-done.8
  85.5 0.8 collective-permute-start.10
  86.2 3.1 %collective-permute-start.11 = (f32[6,8,4,2]{3,0,2,1:T(8,128)S(1)}, f32[6,8,4,2]{3,0,2,1:T(8,128)S(1)}, u32[]{:S(2)}, u32[]{:S(2)}) collective-permute-start(f32[6,8,4,2]{3,0,2,1:T(8,128)S(1)} %get-tuple-element.55), channel_id=1, source_target_pairs={{1,0},{2,1},{3,2},{0,3},{5,4},{6,5},{7,6},{4,7},{9,8},{10,9},{11,1... | collective-permute-start | bytes 4616 | tf_op jit(solution)/shard_map/ppermute | solution.py:21
  89.6 3.3 %collective-permute-done.10 = f32[6,8,4,2]{3,0,2,1:T(8,128)S(1)} collective-permute-done((f32[6,8,4,2]{3,0,2,1:T(8,128)S(1)}, f32[6,8,4,2]{3,0,2,1:T(8,128)S(1)}, u32[]{:S(2)}, u32[]{:S(2)}) %collective-permute-start.10) | collective-permute-done | bytes 1568 | tf_op jit(solution)/shard_map/ppermute | solution.py:19
  94.6 1.0 collective-permute-start.14
  95.5 2.9 %collective-permute-start.15 = (f32[6,12,8,2]{3,1,2,0:T(8,128)S(1)}, f32[6,12,8,2]{3,1,2,0:T(8,128)S(1)}, u32[]{:S(2)}, u32[]{:S(2)}) collective-permute-start(f32[6,12,8,2]{3,1,2,0:T(8,128)S(1)} %get-tuple-element.27), channel_id=1, source_target_pairs={{1,0},{2,1},{3,2},{0,3},{5,4},{6,5},{7,6},{4,7},{9,8},{10,9},{11,1... | collective-permute-start | bytes 13832 | tf_op jit(solution)/shard_map/ppermute | solution.py:21
  98.5 9.9 %collective-permute-done.14 = f32[6,12,8,2]{3,1,2,0:T(8,128)S(1)} collective-permute-done((f32[6,12,8,2]{3,1,2,0:T(8,128)S(1)}, f32[6,12,8,2]{3,1,2,0:T(8,128)S(1)}, u32[]{:S(2)}, u32[]{:S(2)}) %collective-permute-start.14) | collective-permute-done | bytes 4640 | tf_op jit(solution)/shard_map/ppermute | solution.py:19
  108.4 3.8 %collective-permute-done.15 = f32[6,12,8,2]{3,1,2,0:T(8,128)S(1)} collective-permute-done((f32[6,12,8,2]{3,1,2,0:T(8,128)S(1)}, f32[6,12,8,2]{3,1,2,0:T(8,128)S(1)}, u32[]{:S(2)}, u32[]{:S(2)}) %collective-permute-start.15) | collective-permute-done | bytes 4640 | tf_op jit(solution)/shard_map/ppermute | solution.py:21
  113.7 0.6 fusion.56
  115.0 0.8 fusion.6
  116.8 2.7 %copy.136 = f32[6,8,8,128]{0,3,2,1:T(8,128)} copy(f32[6,8,8,128]{3,1,2,0:T(8,128)S(1)} %fusion.93) | data formatting | bytes 393216 | tf_op jit(solution)/shard_map/add | solution.py:98
  119.5 4.8 %reduce_sum.29 = f32[6,4,4,64]{0,3,2,1:T(8,128)S(1)} reduce(f32[6,4,2,4,2,64,2]{0,6,5,4,3,2,1:T(2,128)} %bitcast.126, f32[]{:T(128)} %constant.168.clone.1), dimensions={2,4,6}, to_apply=%region_2.3 | reduce | flops 43008 | bytes 221188 | tf_op jit(solution)/shard_map/reduce_sum | solution.py:129
  124.8 3.9 %collective-permute-start.17 = (f32[6,2,4,64]{3,0,2,1:T(8,128)S(1)}, f32[6,2,4,64]{3,0,2,1:T(8,128)S(1)}, u32[]{:S(2)}, u32[]{:S(2)}) collective-permute-start(f32[6,2,4,64]{3,0,2,1:T(8,128)S(1)} %get-tuple-element.59), channel_id=1, source_target_pairs={{4,0},{8,4},{12,8},{16,12},{20,16},{24,20},{28,24},{0,28},{5,1},{9... | collective-permute-start | bytes 36872 | tf_op jit(solution)/shard_map/ppermute | solution.py:21
  129.1 1.2 collective-permute-done.16
  130.5 0.7 collective-permute-start.18
  131.1 3.2 %collective-permute-start.19 = (f32[6,8,4,2]{3,0,2,1:T(8,128)S(1)}, f32[6,8,4,2]{3,0,2,1:T(8,128)S(1)}, u32[]{:S(2)}, u32[]{:S(2)}) collective-permute-start(f32[6,8,4,2]{3,0,2,1:T(8,128)S(1)} %get-tuple-element.51), channel_id=1, source_target_pairs={{1,0},{2,1},{3,2},{0,3},{5,4},{6,5},{7,6},{4,7},{9,8},{10,9},{11,1... | collective-permute-start | bytes 4616 | tf_op jit(solution)/shard_map/ppermute | solution.py:21
  134.4 0.7 copy.142
  135.1 3.2 %collective-permute-done.18 = f32[6,8,4,2]{3,0,2,1:T(8,128)S(1)} collective-permute-done((f32[6,8,4,2]{3,0,2,1:T(8,128)S(1)}, f32[6,8,4,2]{3,0,2,1:T(8,128)S(1)}, u32[]{:S(2)}, u32[]{:S(2)}) %collective-permute-start.18) | collective-permute-done | bytes 1568 | tf_op jit(solution)/shard_map/ppermute | solution.py:19
  138.3 1.8 %collective-permute-done.19 = f32[6,8,4,2]{3,0,2,1:T(8,128)S(1)} collective-permute-done((f32[6,8,4,2]{3,0,2,1:T(8,128)S(1)}, f32[6,8,4,2]{3,0,2,1:T(8,128)S(1)}, u32[]{:S(2)}, u32[]{:S(2)}) %collective-permute-start.19) | collective-permute-done | bytes 1568 | tf_op jit(solution)/shard_map/ppermute | solution.py:21
  141.6 1.7 %copy.139 = f32[6,8,8,64]{2,1,3,0:T(8,128)} copy(f32[6,8,8,64]{3,1,2,0:T(8,128)S(1)} %bitcast.129) | data formatting | bytes 196608 | tf_op jit(solution)/shard_map/reshape | solution.py:133
  143.3 1.6 %broadcast_in_dim.145 = f32[6,8,8,64,2]{2,1,4,3,0:T(8,128)S(1)} broadcast(f32[6,8,8,64]{2,1,3,0:T(8,128)} %copy.139), dimensions={0,1,2,3} | broadcast | bytes 294912 | tf_op jit(solution)/shard_map/broadcast_in_dim | solution.py:133
  144.9 1.1 copy.140
  146.0 0.7 copy.141
  (190 shorter events, 18.5 us)
Async XLA Ops:
  0.6 10.9 %copy-start.1 = (f32[3,6,6]{2,1,0:T(8,128)S(1)}, f32[3,6,6]{2,1,0:T(8,128)}, u32[]{:S(2)}) copy-start(f32[3,6,6]{2,1,0:T(8,128)} %param.7) | copy-start | bytes 1300
  1.7 11.1 %collective-permute-start = (f32[6,2,8,128]{3,1,2,0:T(2,128)S(1)}, f32[6,2,8,128]{3,1,2,0:T(2,128)S(1)}, u32[]{:S(2)}, u32[]{:S(2)}) collective-permute-start(f32[6,2,8,128]{3,1,2,0:T(2,128)S(1)} %get-tuple-element.42), channel_id=1, source_target_pairs={{0,4},{4,8},{8,12},{12,16},{16,20},{20,24},{24,28},{28,0},{1,5},{5... | collective-permute-start | bytes 147464 | tf_op jit(solution)/shard_map/ppermute | solution.py:19
  2.2 10.6 %collective-permute-start.1 = (f32[6,2,8,128]{3,1,2,0:T(2,128)S(1)}, f32[6,2,8,128]{3,1,2,0:T(2,128)S(1)}, u32[]{:S(2)}, u32[]{:S(2)}) collective-permute-start(f32[6,2,8,128]{3,1,2,0:T(2,128)S(1)} %get-tuple-element.43), channel_id=1, source_target_pairs={{4,0},{8,4},{12,8},{16,12},{20,16},{24,20},{28,24},{0,28},{5,1},{9... | collective-permute-start | bytes 147464 | tf_op jit(solution)/shard_map/ppermute | solution.py:21
  12.2 14.2 %copy-start.2 = (f32[8,8,128]{2,1,0:T(8,128)S(1)}, f32[8,8,128]{2,1,0:T(8,128)}, u32[]{:S(2)}) copy-start(f32[8,8,128]{2,1,0:T(8,128)} %param.6) | copy-start | bytes 98308
  13.1 14.4 %collective-permute-start.2 = (f32[6,12,8,2]{3,1,2,0:T(8,128)S(1)}, f32[6,12,8,2]{3,1,2,0:T(8,128)S(1)}, u32[]{:S(2)}, u32[]{:S(2)}) collective-permute-start(f32[6,12,8,2]{3,1,2,0:T(8,128)S(1)} %get-tuple-element.30), channel_id=1, source_target_pairs={{0,1},{1,2},{2,3},{3,0},{4,5},{5,6},{6,7},{7,4},{8,9},{9,10},{10,1... | collective-permute-start | bytes 13832 | tf_op jit(solution)/shard_map/ppermute | solution.py:19
  15.4 18.1 %collective-permute-start.3 = (f32[6,12,8,2]{3,1,2,0:T(8,128)S(1)}, f32[6,12,8,2]{3,1,2,0:T(8,128)S(1)}, u32[]{:S(2)}, u32[]{:S(2)}) collective-permute-start(f32[6,12,8,2]{3,1,2,0:T(8,128)S(1)} %get-tuple-element.31), channel_id=1, source_target_pairs={{1,0},{2,1},{3,2},{0,3},{5,4},{6,5},{7,6},{4,7},{9,8},{10,9},{11,1... | collective-permute-start | bytes 13832 | tf_op jit(solution)/shard_map/ppermute | solution.py:21
  36.0 2.0 %copy-start = (f32[6,8,8,128]{3,2,1,0:T(8,128)S(1)}, f32[6,8,8,128]{3,2,1,0:T(8,128)}, u32[]{:S(2)}) copy-start(f32[6,8,8,128]{3,2,1,0:T(8,128)} %param.5) | copy-start | bytes 589828
  39.0 4.5 %collective-permute-start.4 = (f32[6,2,8,128]{3,1,2,0:T(2,128)S(1)}, f32[6,2,8,128]{3,1,2,0:T(2,128)S(1)}, u32[]{:S(2)}, u32[]{:S(2)}) collective-permute-start(f32[6,2,8,128]{3,1,2,0:T(2,128)S(1)} %get-tuple-element.38), channel_id=1, source_target_pairs={{0,4},{4,8},{8,12},{12,16},{16,20},{20,24},{24,28},{28,0},{1,5},{5... | collective-permute-start | bytes 147464 | tf_op jit(solution)/shard_map/ppermute | solution.py:19
  39.0 4.4 %collective-permute-start.5 = (f32[6,2,8,128]{3,1,2,0:T(2,128)S(1)}, f32[6,2,8,128]{3,1,2,0:T(2,128)S(1)}, u32[]{:S(2)}, u32[]{:S(2)}) collective-permute-start(f32[6,2,8,128]{3,1,2,0:T(2,128)S(1)} %get-tuple-element.39), channel_id=1, source_target_pairs={{4,0},{8,4},{12,8},{16,12},{20,16},{24,20},{28,24},{0,28},{5,1},{9... | collective-permute-start | bytes 147464 | tf_op jit(solution)/shard_map/ppermute | solution.py:21
  43.7 13.9 %collective-permute-start.6 = (f32[6,12,8,2]{3,1,2,0:T(8,128)S(1)}, f32[6,12,8,2]{3,1,2,0:T(8,128)S(1)}, u32[]{:S(2)}, u32[]{:S(2)}) collective-permute-start(f32[6,12,8,2]{3,1,2,0:T(8,128)S(1)} %get-tuple-element.28), channel_id=1, source_target_pairs={{0,1},{1,2},{2,3},{3,0},{4,5},{5,6},{6,7},{7,4},{8,9},{9,10},{10,1... | collective-permute-start | bytes 13832 | tf_op jit(solution)/shard_map/ppermute | solution.py:19
  44.9 19.9 %collective-permute-start.7 = (f32[6,12,8,2]{3,1,2,0:T(8,128)S(1)}, f32[6,12,8,2]{3,1,2,0:T(8,128)S(1)}, u32[]{:S(2)}, u32[]{:S(2)}) collective-permute-start(f32[6,12,8,2]{3,1,2,0:T(8,128)S(1)} %get-tuple-element.29), channel_id=1, source_target_pairs={{1,0},{2,1},{3,2},{0,3},{5,4},{6,5},{7,6},{4,7},{9,8},{10,9},{11,1... | collective-permute-start | bytes 13832 | tf_op jit(solution)/shard_map/ppermute | solution.py:21
  78.1 16.2 %collective-permute-start.12 = (f32[6,2,8,128]{3,1,2,0:T(2,128)S(1)}, f32[6,2,8,128]{3,1,2,0:T(2,128)S(1)}, u32[]{:S(2)}, u32[]{:S(2)}) collective-permute-start(f32[6,2,8,128]{3,1,2,0:T(2,128)S(1)} %get-tuple-element.34), channel_id=1, source_target_pairs={{0,4},{4,8},{8,12},{12,16},{16,20},{20,24},{24,28},{28,0},{1,5},{5... | collective-permute-start | bytes 147464 | tf_op jit(solution)/shard_map/ppermute | solution.py:19
  78.1 16.2 %collective-permute-start.13 = (f32[6,2,8,128]{3,1,2,0:T(2,128)S(1)}, f32[6,2,8,128]{3,1,2,0:T(2,128)S(1)}, u32[]{:S(2)}, u32[]{:S(2)}) collective-permute-start(f32[6,2,8,128]{3,1,2,0:T(2,128)S(1)} %get-tuple-element.35), channel_id=1, source_target_pairs={{4,0},{8,4},{12,8},{16,12},{20,16},{24,20},{28,24},{0,28},{5,1},{9... | collective-permute-start | bytes 147464 | tf_op jit(solution)/shard_map/ppermute | solution.py:21
  81.0 4.3 %collective-permute-start.8 = (f32[6,2,4,64]{3,0,2,1:T(8,128)S(1)}, f32[6,2,4,64]{3,0,2,1:T(8,128)S(1)}, u32[]{:S(2)}, u32[]{:S(2)}) collective-permute-start(f32[6,2,4,64]{3,0,2,1:T(8,128)S(1)} %get-tuple-element.62), channel_id=1, source_target_pairs={{0,4},{4,8},{8,12},{12,16},{16,20},{20,24},{24,28},{28,0},{1,5},{5... | collective-permute-start | bytes 36872 | tf_op jit(solution)/shard_map/ppermute | solution.py:19
  81.1 4.2 %collective-permute-start.9 = (f32[6,2,4,64]{3,0,2,1:T(8,128)S(1)}, f32[6,2,4,64]{3,0,2,1:T(8,128)S(1)}, u32[]{:S(2)}, u32[]{:S(2)}) collective-permute-start(f32[6,2,4,64]{3,0,2,1:T(8,128)S(1)} %get-tuple-element.63), channel_id=1, source_target_pairs={{4,0},{8,4},{12,8},{16,12},{20,16},{24,20},{28,24},{0,28},{5,1},{9... | collective-permute-start | bytes 36872 | tf_op jit(solution)/shard_map/ppermute | solution.py:21
  85.5 7.5 %collective-permute-start.10 = (f32[6,8,4,2]{3,0,2,1:T(8,128)S(1)}, f32[6,8,4,2]{3,0,2,1:T(8,128)S(1)}, u32[]{:S(2)}, u32[]{:S(2)}) collective-permute-start(f32[6,8,4,2]{3,0,2,1:T(8,128)S(1)} %get-tuple-element.54), channel_id=1, source_target_pairs={{0,1},{1,2},{2,3},{3,0},{4,5},{5,6},{6,7},{7,4},{8,9},{9,10},{10,1... | collective-permute-start | bytes 4616 | tf_op jit(solution)/shard_map/ppermute | solution.py:19
  86.2 6.8 %collective-permute-start.11 = (f32[6,8,4,2]{3,0,2,1:T(8,128)S(1)}, f32[6,8,4,2]{3,0,2,1:T(8,128)S(1)}, u32[]{:S(2)}, u32[]{:S(2)}) collective-permute-start(f32[6,8,4,2]{3,0,2,1:T(8,128)S(1)} %get-tuple-element.55), channel_id=1, source_target_pairs={{1,0},{2,1},{3,2},{0,3},{5,4},{6,5},{7,6},{4,7},{9,8},{10,9},{11,1... | collective-permute-start | bytes 4616 | tf_op jit(solution)/shard_map/ppermute | solution.py:21
  94.6 13.8 %collective-permute-start.14 = (f32[6,12,8,2]{3,1,2,0:T(8,128)S(1)}, f32[6,12,8,2]{3,1,2,0:T(8,128)S(1)}, u32[]{:S(2)}, u32[]{:S(2)}) collective-permute-start(f32[6,12,8,2]{3,1,2,0:T(8,128)S(1)} %get-tuple-element.26), channel_id=1, source_target_pairs={{0,1},{1,2},{2,3},{3,0},{4,5},{5,6},{6,7},{7,4},{8,9},{9,10},{10,1... | collective-permute-start | bytes 13832 | tf_op jit(solution)/shard_map/ppermute | solution.py:19
  95.5 16.7 %collective-permute-start.15 = (f32[6,12,8,2]{3,1,2,0:T(8,128)S(1)}, f32[6,12,8,2]{3,1,2,0:T(8,128)S(1)}, u32[]{:S(2)}, u32[]{:S(2)}) collective-permute-start(f32[6,12,8,2]{3,1,2,0:T(8,128)S(1)} %get-tuple-element.27), channel_id=1, source_target_pairs={{1,0},{2,1},{3,2},{0,3},{5,4},{6,5},{7,6},{4,7},{9,8},{10,9},{11,1... | collective-permute-start | bytes 13832 | tf_op jit(solution)/shard_map/ppermute | solution.py:21
  124.7 5.5 %collective-permute-start.16 = (f32[6,2,4,64]{3,0,2,1:T(8,128)S(1)}, f32[6,2,4,64]{3,0,2,1:T(8,128)S(1)}, u32[]{:S(2)}, u32[]{:S(2)}) collective-permute-start(f32[6,2,4,64]{3,0,2,1:T(8,128)S(1)} %get-tuple-element.58), channel_id=1, source_target_pairs={{0,4},{4,8},{8,12},{12,16},{16,20},{20,24},{24,28},{28,0},{1,5},{5... | collective-permute-start | bytes 36872 | tf_op jit(solution)/shard_map/ppermute | solution.py:19
  124.8 5.5 %collective-permute-start.17 = (f32[6,2,4,64]{3,0,2,1:T(8,128)S(1)}, f32[6,2,4,64]{3,0,2,1:T(8,128)S(1)}, u32[]{:S(2)}, u32[]{:S(2)}) collective-permute-start(f32[6,2,4,64]{3,0,2,1:T(8,128)S(1)} %get-tuple-element.59), channel_id=1, source_target_pairs={{4,0},{8,4},{12,8},{16,12},{20,16},{24,20},{28,24},{0,28},{5,1},{9... | collective-permute-start | bytes 36872 | tf_op jit(solution)/shard_map/ppermute | solution.py:21
  130.5 7.8 %collective-permute-start.18 = (f32[6,8,4,2]{3,0,2,1:T(8,128)S(1)}, f32[6,8,4,2]{3,0,2,1:T(8,128)S(1)}, u32[]{:S(2)}, u32[]{:S(2)}) collective-permute-start(f32[6,8,4,2]{3,0,2,1:T(8,128)S(1)} %get-tuple-element.50), channel_id=1, source_target_pairs={{0,1},{1,2},{2,3},{3,0},{4,5},{5,6},{6,7},{7,4},{8,9},{9,10},{10,1... | collective-permute-start | bytes 4616 | tf_op jit(solution)/shard_map/ppermute | solution.py:19
  131.1 9.0 %collective-permute-start.19 = (f32[6,8,4,2]{3,0,2,1:T(8,128)S(1)}, f32[6,8,4,2]{3,0,2,1:T(8,128)S(1)}, u32[]{:S(2)}, u32[]{:S(2)}) collective-permute-start(f32[6,8,4,2]{3,0,2,1:T(8,128)S(1)} %get-tuple-element.51), channel_id=1, source_target_pairs={{1,0},{2,1},{3,2},{0,3},{5,4},{6,5},{7,6},{4,7},{9,8},{10,9},{11,1... | collective-permute-start | bytes 4616 | tf_op jit(solution)/shard_map/ppermute | solution.py:21
where the time goes:
time: 147 us
  waiting for transfers between devices  49.8 us (34%)
  starting transfers between devices  35.5 us (24%)
  other arithmetic  21.6 us (15%)
  local copies, waits for them, and re-layouts  21.4 us (15%)
  between operations  10.8 us (7%)
  matrix products  7.59 us (5%)
    ppermute x10, waiting for transfers between devices, extended(): lax.ppermute(tail, axis, [(i, (i + 1) % count) for i in range(count)])  30.7 us
    ppermute x10, starting transfers between devices, extended(): lax.ppermute(head, axis, [((i + 1) % count, i) for i in range(count)])  28.8 us
    ppermute x10, waiting for transfers between devices, extended(): lax.ppermute(head, axis, [((i + 1) % count, i) for i in range(count)])  19.1 us
    reduce_sum x3, other arithmetic, restrict(): return reshaped.mean(axis=(-5, -3, -1))  9.89 us
    dot_general x15, matrix products, flux_of(): jnp.einsum('uv,vijk->uijk', coupling[direction], padded, precision=PRECISE)  7.59 us
    ppermute x10, starting transfers between devices, extended(): lax.ppermute(tail, axis, [(i, (i + 1) % count) for i in range(count)])  6.68 us
    add x15, other arithmetic, divergence(): 0.5 * (cut_axis(fluxes, 1, face_count) + cut_axis(fluxes, 2, face_count))  3.56 us
  transfers between devices with their start and end apart: 20, of which 14 were waited for; matrix products, arithmetic and copies ran while one was open for 8% of the time, Pallas kernels for 0%

commit v1 on v0

v1 whole, which is shorter than its diff:
```python
import functools

import jax
import jax.numpy as jnp
from jax import lax
from jax.experimental import pallas as pl
from jax.experimental.pallas import tpu as pltpu
from jax.sharding import PartitionSpec as P

NEAR = -0.13
FAR = 0.02
CENTRE = 0.66
FIRST = 0.4
NV = 6


def kernel(
    nb, ns, coup, ftype, frot, q_hbm, dt_hbm, upd_hbm, res_hbm,
    q0, s1, s2, dt, acc, cacc, racc, rst, res, cs, c1, cst, upd,
    pf_s, pf_r, hf_r, pc_s, pc_r, hc_s, hc_r,
    loc, hs_sem, hr_sem, ks_sem, kr_sem,
):
    rows, nj, nk = dt.shape
    crows = rows // 2
    blk, sub = lax.axis_index("blk"), lax.axis_index("sub")
    nxt, prv = lax.rem(blk + 1, nb), lax.rem(blk + nb - 1, nb)
    right, left = lax.rem(sub + 1, ns), lax.rem(sub + ns - 1, ns)
    has_left, has_right = sub > 0, sub < ns - 1

    load_q = pltpu.make_async_copy(q_hbm, q0.at[:, pl.ds(2, rows)], loc.at[0])
    load_t = pltpu.make_async_copy(dt_hbm, dt, loc.at[1])
    load_q.start()
    load_t.start()

    barrier = pltpu.get_barrier_semaphore()
    pl.semaphore_signal(barrier, inc=1, device_id={"blk": nxt})
    pl.semaphore_signal(barrier, inc=1, device_id={"blk": prv})

    @pl.when(has_left)
    def _():
        pl.semaphore_signal(barrier, inc=1, device_id={"sub": left})

    @pl.when(has_right)
    def _():
        pl.semaphore_signal(barrier, inc=1, device_id={"sub": right})

    shape = (nj, nk)
    jj = lax.broadcasted_iota(jnp.int32, shape, 0)
    kk = lax.broadcasted_iota(jnp.int32, shape, 1)

    def splat(ref, side):
        return jnp.full(shape, ref[0, side], jnp.int32)

    kinds = [splat(ftype, side) for side in (0, 1)]
    rots = [splat(frot, side) for side in (0, 1)]

    def hcoup(d, u, v):
        return 0.5 * coup[d, u, v]

    def half_flux(x, d):
        s = 0.25 * x[1 + d]
        out = []
        for u in range(NV):
            total = s * x[u]
            for v in range(NV):
                total = total + hcoup(d, u, v) * x[v]
            out.append(total)
        return out

    def roll(x, shift, axis):
        return pltpu.roll(x, shift % x.shape[axis], axis)

    def zero_ends(ref, n):
        for v in range(NV):
            for i in (0, 1, n + 2, n + 3):
                ref[v, i] = jnp.zeros(shape, jnp.float32)

    def own_part(ref, out, n, h):
        step = 2
        j3 = lax.broadcasted_iota(jnp.int32, (step, nj, nk), 1)

        def row(t, carry):
            i0 = t * step

            def at(v, off):
                return ref[v, pl.ds(i0 + 2 + off, step)]

            q = [at(v, 0) for v in range(NV)]
            damp, diffs, sides = [], [], []
            ip = [at(v, 1) for v in range(NV)]
            im = [at(v, -1) for v in range(NV)]
            kp = [roll(x, -h, 2) for x in q]
            km = [roll(x, h, 2) for x in q]
            rp = [roll(x, -h, 1) for x in q]
            rm = [roll(x, h, 1) for x in q]
            jp, jm = [], []
            for v in range(NV):
                sign = -1.0 if v == 2 else 1.0
                edge = sign * q[v] if v == 2 else q[v]
                jp.append(jnp.where(j3 >= nj - h, edge, rp[v]))
                jm.append(jnp.where(j3 < h, edge, rm[v]))
                swap_hi = jnp.where(j3 < nj - h, rp[v], rm[v])
                swap_lo = jnp.where(j3 < h, rp[v], rm[v])
                if v == 2:
                    swap_hi, swap_lo = -swap_hi, -swap_lo
                jpp = jnp.where(j3 < nj - 2 * h, roll(q[v], -2 * h, 1), swap_hi)
                jmm = jnp.where(j3 >= 2 * h, roll(q[v], 2 * h, 1), swap_lo)
                near = ((ip[v] + im[v]) + (jp[v] + jm[v])) + (kp[v] + km[v])
                far = ((at(v, 2) + at(v, -2)) + (jpp + jmm)) + (
                    roll(q[v], -2 * h, 2) + roll(q[v], 2 * h, 2)
                )
                damp.append(CENTRE * q[v] + NEAR * near + FAR * far)
            for d, (p, m) in enumerate(((ip, im), (jp, jm), (kp, km))):
                sp, sm = 0.25 * p[1 + d], 0.25 * m[1 + d]
                diff = [p[v] - m[v] for v in range(NV)]
                for u in range(NV):
                    total = sp * p[u] - sm * m[u]
                    for v in range(NV):
                        total = total + hcoup(d, u, v) * diff[v]
                    damp[u] = damp[u] + total
            for u in range(NV):
                out[u, pl.ds(i0, step)] = damp[u]
            return carry

        lax.fori_loop(0, n // step, row, 0)

    def pack(ref, dst, n, h):
        group = kk // (4 * h)
        packed = []
        for v in range(NV):
            p = roll(ref[v, 2], 2 * h, 1)
            for i in range(1, n):
                p = jnp.where(group == i, roll(ref[v, 2 + i], 2 * h + 4 * h * i, 1), p)
            dst[v] = p
            packed.append(p)
        return packed

    def k_edges(low, high, h):
        r = kk % (4 * h)
        near = [jnp.where(r < 2 * h, low[v], high[v]) for v in range(NV)]
        hf = half_flux(near, 2)
        out = []
        for v in range(NV):
            e = jnp.where(r < 2 * h, -hf[v], hf[v]) + NEAR * near[v]
            far = FAR * jnp.where(r < 2 * h, roll(high[v], -2 * h, 1), roll(low[v], 2 * h, 1))
            inner = jnp.where(r < 2 * h, roll(e, -h, 1), roll(e, h, 1))
            out.append(far + jnp.where((r >= h) & (r < 3 * h), inner, 0.0))
        return out

    def k_correction(own, ref, h):
        low = [jnp.where(jnp.full(shape, sub) > 0, ref[0, v], 0.0) for v in range(NV)]
        high = [jnp.where(jnp.full(shape, sub) < ns - 1, ref[1, v], 0.0) for v in range(NV)]
        got = k_edges(low, high, h)
        return [got[v] - own[v] for v in range(NV)]

    def flip(x):
        bit = 1
        while bit < nj:
            x = jnp.where((jj & bit) == 0, roll(x, -bit, 0), roll(x, bit, 0))
            bit *= 2
        return x

    def ghost(side, same, other, own):
        kind, rot = kinds[side], rots[side]
        out = []
        for v in range(NV):
            wall = -own[v] if v == 1 else own[v]
            g = jnp.where(
                kind == 0, same[v], jnp.where(kind == 1, other[v], jnp.where(kind == 2, wall, 0.0))
            )
            out.append(jnp.where((rot & 1) == 1, flip(g), g))
        turn = ((rot >> 1) & 1) == 1
        out[2], out[3] = jnp.where(turn, -out[3], out[2]), jnp.where(turn, out[2], out[3])
        return out

    def i_edges(before, after, ref, n):
        own = lambda i: [ref[v, 2 + i] for v in range(NV)]
        lo_near = ghost(0, before[1], after[0], own(0))
        lo_far = ghost(0, before[0], after[1], own(1))
        hi_near = ghost(1, after[0], before[1], own(n - 1))
        hi_far = ghost(1, after[1], before[0], own(n - 2))
        lo_f, hi_f = half_flux(lo_near, 0), half_flux(hi_near, 0)
        each = range(NV)
        return {
            0: [FAR * lo_far[v] + NEAR * lo_near[v] - lo_f[v] for v in each],
            1: [FAR * lo_near[v] for v in each],
            n - 1: [FAR * hi_far[v] + NEAR * hi_near[v] + hi_f[v] for v in each],
            n - 2: [FAR * hi_near[v] for v in each],
        }

    def finish(out, n, h, kc, edges, then, order):
        mask = (kk < 2 * h) | (kk >= nk - 2 * h)
        for i in order:
            for v in range(NV):
                r = out[v, i] + jnp.where(mask, roll(kc[v], -(2 * h + 4 * h * i), 1), 0.0)
                if i in edges:
                    r = r + edges[i][v]
                then(v, i, r)

    def pair_sum(x):
        x = x + jnp.where((kk & 1) == 0, roll(x, -1, 1), roll(x, 1, 1))
        return x + jnp.where((jj & 1) == 0, roll(x, -1, 0), roll(x, 1, 0))

    def blk_copies(number, to_next, to_prev, dst):
        made = []
        for side, (src, who) in enumerate(((to_next, nxt), (to_prev, prv))):
            made.append(
                pltpu.make_async_remote_copy(
                    src_ref=src, dst_ref=dst.at[side],
                    send_sem=hs_sem.at[number, side], recv_sem=hr_sem.at[number, side],
                    device_id={"blk": who},
                )
            )
        return made

    def sub_copies(number, src, dst):
        made = []
        for side, who in enumerate((right, left)):
            made.append(
                pltpu.make_async_remote_copy(
                    src_ref=src, dst_ref=dst.at[side],
                    send_sem=ks_sem.at[number, side], recv_sem=kr_sem.at[number, side],
                    device_id={"sub": who},
                )
            )
        return made

    def go(copies):
        for c in copies:
            c.start()

    def sub_go(copies):
        pl.when(has_right)(copies[0].start)
        pl.when(has_left)(copies[1].start)

    def got(copies):
        for c in copies:
            c.wait_recv()

    def sub_got(copies):
        pl.when(has_left)(copies[0].wait_recv)
        pl.when(has_right)(copies[1].wait_recv)

    def sent(copies):
        for c in copies:
            c.wait_send()

    def sub_sent(copies):
        pl.when(has_right)(copies[0].wait_send)
        pl.when(has_left)(copies[1].wait_send)

    def fine_halo(number):
        read = lambda side: [[hf_r[number, side, v, r] for v in range(NV)] for r in (0, 1)]
        return read(0), read(1)

    def coarse_halo(number):
        def read(side):
            x = [hc_r[number, side, v] for v in range(NV)]
            even = (jj & 1) == 0
            return [
                [jnp.where(even, y, roll(y, 1, 0)) for y in x],
                [jnp.where(even, roll(y, -1, 0), y) for y in x],
            ]
        return read(0), read(1)

    def coarse_rows(number, ref):
        even = (jj & 1) == 0
        for v in range(NV):
            hc_s[number, 0, v] = jnp.where(even, ref[v, crows], ref[v, crows + 1])
            hc_s[number, 1, v] = jnp.where(even, ref[v, 2], ref[v, 3])

    edge_first = [0, 1, rows - 2, rows - 1] + list(range(2, rows - 2))
    every = []

    zero_ends(q0, rows)
    zero_ends(s1, rows)
    zero_ends(s2, rows)
    zero_ends(cs, crows)
    zero_ends(c1, crows)
    ends = jnp.where(has_left, 0, 1) + jnp.where(has_right, 0, 1)
    pl.semaphore_wait(barrier, 4 - ends)
    h0 = blk_copies(0, q_hbm.at[:, pl.ds(rows - 2, 2)], q_hbm.at[:, pl.ds(0, 2)], hf_r.at[0])
    go(h0)
    load_q.wait()
    load_t.wait()
    own = k_edges(*[pack(q0, pf_s.at[0], rows, 1)] * 2, 1)
    k0 = sub_copies(0, pf_s.at[0], pf_r.at[0])
    sub_go(k0)
    own_part(q0, acc, rows, 1)
    for i in range(crows):
        cst[i] = 0.125 * pair_sum(dt[2 * i] + dt[2 * i + 1])
    sub_got(k0)
    kc = k_correction(own, pf_r.at[0], 1)
    got(h0)
    before, after = fine_halo(0)

    def store1(v, i, r):
        s1[v, 2 + i] = q0[v, 2 + i] - FIRST * dt[i] * r

    finish(acc, rows, 1, kc, i_edges(before, after, q0, rows), store1, edge_first)

    h1 = blk_copies(1, s1.at[:, pl.ds(rows, 2)], s1.at[:, pl.ds(2, 2)], hf_r.at[1])
    go(h1)
    own = k_edges(*[pack(s1, pf_s.at[1], rows, 1)] * 2, 1)
    k1 = sub_copies(1, pf_s.at[1], pf_r.at[1])
    sub_go(k1)
    own_part(s1, acc, rows, 1)
    sub_got(k1)
    kc = k_correction(own, pf_r.at[1], 1)
    got(h1)
    before, after = fine_halo(1)

    def store2(v, i, r):
        s2[v, 2 + i] = q0[v, 2 + i] - dt[i] * r

    finish(acc, rows, 1, kc, i_edges(before, after, s1, rows), store2, edge_first)

    h2 = blk_copies(2, s2.at[:, pl.ds(rows, 2)], s2.at[:, pl.ds(2, 2)], hf_r.at[2])
    go(h2)
    own = k_edges(*[pack(s2, pf_s.at[2], rows, 1)] * 2, 1)
    k2 = sub_copies(2, pf_s.at[2], pf_r.at[2])
    sub_go(k2)
    for v in range(NV):
        for i in range(crows):
            cs[v, 2 + i] = 0.125 * pair_sum(s2[v, 2 + 2 * i] + s2[v, 3 + 2 * i])
    coarse_rows(0, cs)
    h3 = blk_copies(3, hc_s.at[0, 0], hc_s.at[0, 1], hc_r.at[0])
    go(h3)
    own_c = k_edges(*[pack(cs, pc_s.at[0], crows, 2)] * 2, 2)
    k3 = sub_copies(3, pc_s.at[0], pc_r.at[0])
    sub_go(k3)
    own_part(s2, acc, rows, 1)
    sub_got(k2)
    kc = k_correction(own, pf_r.at[2], 1)
    got(h2)
    before, after = fine_halo(2)

    def store3(v, i, r):
        res[v, i] = r

    finish(acc, rows, 1, kc, i_edges(before, after, s2, rows), store3, edge_first)
    for v in range(NV):
        for i in range(crows):
            r = 0.125 * pair_sum(res[v, 2 * i] + res[v, 2 * i + 1])
            rst[v, i] = r
            c1[v, 2 + i] = cs[v, 2 + i] - FIRST * cst[i] * r

    coarse_rows(1, c1)
    h4 = blk_copies(4, hc_s.at[1, 0], hc_s.at[1, 1], hc_r.at[1])
    go(h4)
    own_d = k_edges(*[pack(c1, pc_s.at[1], crows, 2)] * 2, 2)
    k4 = sub_copies(4, pc_s.at[1], pc_r.at[1])
    sub_go(k4)
    out_r = pltpu.make_async_copy(res, res_hbm, loc.at[2])
    out_r.start()
    own_part(cs, cacc, crows, 2)
    sub_got(k3)
    kc = k_correction(own_c, pc_r.at[0], 2)
    got(h3)
    before, after = coarse_halo(0)

    def store4(v, i, r):
        rst[v, i] = r - rst[v, i]

    every_row = list(range(crows))
    finish(cacc, crows, 2, kc, i_edges(before, after, cs, crows), store4, every_row)
    own_part(c1, racc, crows, 2)
    sub_got(k4)
    kc = k_correction(own_d, pc_r.at[1], 2)
    got(h4)
    before, after = coarse_halo(1)

    def store5(v, i, r):
        change = cst[i] * (r - rst[v, i])
        for ii in (2 * i, 2 * i + 1):
            upd[v, ii] = s2[v, 2 + ii] - change

    finish(racc, crows, 2, kc, i_edges(before, after, c1, crows), store5, every_row)
    out_u = pltpu.make_async_copy(upd, upd_hbm, loc.at[3])
    out_u.start()
    for c in (h0, h1, h2, h3, h4):
        sent(c)
    for c in (k0, k1, k2, k3, k4):
        sub_sent(c)
    out_r.wait()
    out_u.wait()


def solution(mesh):
    nb, ns = mesh.shape["blk"], mesh.shape["sub"]

    def body(flow_state, timestep, coupling, face_type, face_rot):
        nv, rows, nj, nk = flow_state.shape
        f32 = jnp.float32
        half = rows // 2
        any_spec = pl.BlockSpec(memory_space=pl.ANY)
        smem = pl.BlockSpec(memory_space=pltpu.SMEM)
        vm = lambda *s: pltpu.VMEM(s + (nj, nk), f32)
        out = jax.ShapeDtypeStruct(flow_state.shape, f32)
        return pl.pallas_call(
            functools.partial(kernel, nb, ns),
            out_shape=(out, out),
            in_specs=[smem, smem, smem, any_spec, any_spec],
            out_specs=(any_spec, any_spec),
            scratch_shapes=[
                vm(nv, rows + 4), vm(nv, rows + 4), vm(nv, rows + 4), vm(rows),
                vm(nv, rows), vm(nv, half), vm(nv, half), vm(nv, half), vm(nv, rows),
                vm(nv, half + 4), vm(nv, half + 4), vm(half), vm(nv, rows),
                vm(3, nv), vm(3, 2, nv), vm(3, 2, nv, 2),
                vm(2, nv), vm(2, 2, nv), vm(2, 2, nv), vm(2, 2, nv),
                pltpu.SemaphoreType.DMA((4,)),
                pltpu.SemaphoreType.DMA((5, 2)), pltpu.SemaphoreType.DMA((5, 2)),
                pltpu.SemaphoreType.DMA((5, 2)), pltpu.SemaphoreType.DMA((5, 2)),
            ],
            compiler_params=pltpu.CompilerParams(collective_id=0, has_side_effects=True),
        )(coupling, face_type, face_rot, flow_state, timestep)

    return jax.shard_map(
        body,
        mesh=mesh,
        in_specs=(
            P(None, "blk", None, "sub"),
            P("blk", None, "sub"),
            P(),
            P("blk", None),
            P("blk", None),
        ),
        out_specs=(P(None, "blk", None, "sub"), P(None, "blk", None, "sub")),
        check_vma=False,
    )
```

time: 147 us -> 22.7 us (0.15)
  waiting for transfers between devices: 49.8 us -> 0 us
  starting transfers between devices: 35.5 us -> 0 us
  other arithmetic: 21.6 us -> 0 us
  Pallas kernels: 0 us -> 19.5 us
  local copies, waits for them, and re-layouts: 21.4 us -> 2.34 us
  between operations: 10.8 us -> 0.65 us
  matrix products: 7.59 us -> 0 us
    ppermute x20 -> x0, waiting for transfers between devices: 49.8 us -> none  [the longest x10 30.7 us: extended(): lax.ppermute(tail, axis, [(i, (i + 1) % count) for i in range(count)])]
    ppermute x20 -> x0, starting transfers between devices: 35.5 us -> none  [the longest x10 28.8 us: extended(): lax.ppermute(head, axis, [((i + 1) % count, i) for i in range(count)])]
    pallas_call x0 -> x1, Pallas kernels: none -> 19.5 us  [body(): pl.pallas_call(functools.partial(kernel, nb, ns), out_shape=(out, out), i...]
    reduce_sum x3 -> x0, other arithmetic: 9.89 us -> none  [restrict(): return reshaped.mean(axis=(-5, -3, -1))]
    dot_general x15 -> x0, matrix products: 7.59 us -> none  [flux_of(): jnp.einsum('uv,vijk->uijk', coupling[direction], padded, precision=PRECISE)]
    add x26 -> x0, other arithmetic: 5.88 us -> none  [the longest x15 3.56 us: divergence(): 0.5 * (cut_axis(fluxes, 1, face_count) + cut_axis(fluxes, 2, face_count))]
    reshape x3 -> x0, local copies, waits for them, and re-layouts: 5.63 us -> none  [the longest x1 2.84 us: restrict(): array.reshape(leading + (shape_of[-3] // 2, 2, shape_of[-2] // 2, 2, shap...]
    slice x35 -> x0, local copies, waits for them, and re-layouts: 4.44 us -> none  [the longest x1 1.37 us: from_halo(): face_rot[0, 1]]
  transfers between devices with their start and end apart: 20 -> 0, of which waited for: 14 -> 0; matrix products, arithmetic and copies ran while one was open for 8% -> 0% of each run, Pallas kernels for 0% -> 0%
where the time goes in v1:
time: 22.7 us; the launch traced here: 22.5 us
  Pallas kernels  19.5 us (86%)
  local copies, waits for them, and re-layouts  2.34 us (10%)
  between operations  0.65 us (3%)
    pallas_call x1, Pallas kernels, body(): pl.pallas_call(functools.partial(kernel, nb, ns), out_shape=(out, out), i...  19.5 us
    unnamed x4, local copies, waits for them, and re-layouts  2.34 us

profile of v1, /device:TPU:0, one launch (start us, length us, event | category | flops | bytes accessed | tf_op | source)
XLA Modules:
  0.0 22.5 jit_solution(7316021347236150070)
XLA Ops:
  0.6 19.5 %shard_map.68 = (f32[6,8,8,128]{3,2,1,0:T(8,128)}, f32[6,8,8,128]{3,2,1,0:T(8,128)}) custom-call(f32[3,6,6]{2,1,0:T(8,128)} %coup.1, s32[1,2]{1,0:T(1,128)} %ftype.1, s32[1,2]{1,0:T(1,128)} %frot.1, f32[6,8,8,128]{3,2,1,0:T(8,128)} %q_hbm.1, f32[8,8,128]{2,1,0:T(8,128)} %dt_hbm.1), custom_call_target="tpu_custom_call" | custom-call | tf_op jit(solution)/shard_map/pallas_call | solution.py:400
  20.1 0.0 copy-start
  20.1 1.7 %copy.9 = f32[6,8,8,128]{3,2,1,0:T(8,128)} copy(f32[6,8,8,128]{3,2,1,0:T(8,128)} %get-tuple-element.4) | data formatting | bytes 393216
  21.8 0.0 copy-done
  21.8 0.7 %copy.10 = f32[6,8,8,128]{3,2,1,0:T(8,128)} copy(f32[6,8,8,128]{3,2,1,0:T(8,128)S(1)} %copy-done) | data formatting | bytes 393216
Async XLA Ops:
  20.1 1.7 %copy-start = (f32[6,8,8,128]{3,2,1,0:T(8,128)S(1)}, f32[6,8,8,128]{3,2,1,0:T(8,128)}, u32[]{:S(2)}) copy-start(f32[6,8,8,128]{3,2,1,0:T(8,128)} %get-tuple-element.5) | copy-start | bytes 589828

commit v2 on v1

--- a/solution.py
+++ b/solution.py
@@ -15,8 +15,8 @@
 
 
 def kernel(
-    nb, ns, coup, ftype, frot, q_hbm, dt_hbm, upd_hbm, res_hbm,
-    q0, s1, s2, dt, acc, cacc, racc, rst, res, cs, c1, cst, upd,
+    nb, ns, coup_hbm, ftype_hbm, frot_hbm, q_hbm, dt_hbm, upd, res,
+    coup, ftype, frot, q0, s1, s2, dt, acc, cacc, racc, rst, cs, c1, cst,
     pf_s, pf_r, hf_r, pc_s, pc_r, hc_s, hc_r,
     loc, hs_sem, hr_sem, ks_sem, kr_sem,
 ):
@@ -29,8 +29,9 @@
 
     load_q = pltpu.make_async_copy(q_hbm, q0.at[:, pl.ds(2, rows)], loc.at[0])
     load_t = pltpu.make_async_copy(dt_hbm, dt, loc.at[1])
-    load_q.start()
-    load_t.start()
+    loads = [load_q, load_t]
+    for n, (src, dst) in enumerate(((coup_hbm, coup), (ftype_hbm, ftype), (frot_hbm, frot))):
+        loads.append(pltpu.make_async_copy(src, dst, loc.at[2 + n]))
 
     barrier = pltpu.get_barrier_semaphore()
     pl.semaphore_signal(barrier, inc=1, device_id={"blk": nxt})
@@ -44,6 +45,9 @@
     def _():
         pl.semaphore_signal(barrier, inc=1, device_id={"sub": right})
 
+    for load in loads:
+        load.start()
+
     shape = (nj, nk)
     jj = lax.broadcasted_iota(jnp.int32, shape, 0)
     kk = lax.broadcasted_iota(jnp.int32, shape, 1)
@@ -51,8 +55,6 @@
     def splat(ref, side):
         return jnp.full(shape, ref[0, side], jnp.int32)
 
-    kinds = [splat(ftype, side) for side in (0, 1)]
-    rots = [splat(frot, side) for side in (0, 1)]
 
     def hcoup(d, u, v):
         return 0.5 * coup[d, u, v]
@@ -278,11 +280,14 @@
     zero_ends(cs, crows)
     zero_ends(c1, crows)
     ends = jnp.where(has_left, 0, 1) + jnp.where(has_right, 0, 1)
+    load_q.wait()
     pl.semaphore_wait(barrier, 4 - ends)
-    h0 = blk_copies(0, q_hbm.at[:, pl.ds(rows - 2, 2)], q_hbm.at[:, pl.ds(0, 2)], hf_r.at[0])
+    h0 = blk_copies(0, q0.at[:, pl.ds(rows, 2)], q0.at[:, pl.ds(2, 2)], hf_r.at[0])
     go(h0)
-    load_q.wait()
-    load_t.wait()
+    for load in loads[1:]:
+        load.wait()
+    kinds = [splat(ftype, side) for side in (0, 1)]
+    rots = [splat(frot, side) for side in (0, 1)]
     own = k_edges(*[pack(q0, pf_s.at[0], rows, 1)] * 2, 1)
     k0 = sub_copies(0, pf_s.at[0], pf_r.at[0])
     sub_go(k0)
@@ -351,8 +356,6 @@
     own_d = k_edges(*[pack(c1, pc_s.at[1], crows, 2)] * 2, 2)
     k4 = sub_copies(4, pc_s.at[1], pc_r.at[1])
     sub_go(k4)
-    out_r = pltpu.make_async_copy(res, res_hbm, loc.at[2])
-    out_r.start()
     own_part(cs, cacc, crows, 2)
     sub_got(k3)
     kc = k_correction(own_c, pc_r.at[0], 2)
@@ -376,14 +379,21 @@
             upd[v, ii] = s2[v, 2 + ii] - change
 
     finish(racc, crows, 2, kc, i_edges(before, after, c1, crows), store5, every_row)
-    out_u = pltpu.make_async_copy(upd, upd_hbm, loc.at[3])
-    out_u.start()
     for c in (h0, h1, h2, h3, h4):
         sent(c)
     for c in (k0, k1, k2, k3, k4):
         sub_sent(c)
-    out_r.wait()
-    out_u.wait()
+
+
+def write_out(upd, res, upd_hbm, res_hbm, sems):
+    copies = [
+        pltpu.make_async_copy(upd, upd_hbm, sems.at[0]),
+        pltpu.make_async_copy(res, res_hbm, sems.at[1]),
+    ]
+    for c in copies:
+        c.start()
+    for c in copies:
+        c.wait()
 
 
 def solution(mesh):
@@ -394,26 +404,36 @@
         f32 = jnp.float32
         half = rows // 2
         any_spec = pl.BlockSpec(memory_space=pl.ANY)
-        smem = pl.BlockSpec(memory_space=pltpu.SMEM)
         vm = lambda *s: pltpu.VMEM(s + (nj, nk), f32)
         out = jax.ShapeDtypeStruct(flow_state.shape, f32)
-        return pl.pallas_call(
+        held = pltpu.VMEM(flow_state.shape, f32)
+        vmem = pl.BlockSpec(memory_space=pltpu.VMEM)
+        made = pl.pallas_call(
             functools.partial(kernel, nb, ns),
-            out_shape=(out, out),
-            in_specs=[smem, smem, smem, any_spec, any_spec],
-            out_specs=(any_spec, any_spec),
+            out_shape=(held, held),
+            in_specs=[any_spec] * 5,
+            out_specs=(vmem, vmem),
             scratch_shapes=[
+                pltpu.SMEM(coupling.shape, f32),
+                pltpu.SMEM(face_type.shape, jnp.int32), pltpu.SMEM(face_rot.shape, jnp.int32),
                 vm(nv, rows + 4), vm(nv, rows + 4), vm(nv, rows + 4), vm(rows),
-                vm(nv, rows), vm(nv, half), vm(nv, half), vm(nv, half), vm(nv, rows),
-                vm(nv, half + 4), vm(nv, half + 4), vm(half), vm(nv, rows),
+                vm(nv, rows), vm(nv, half), vm(nv, half), vm(nv, half),
+                vm(nv, half + 4), vm(nv, half + 4), vm(half),
                 vm(3, nv), vm(3, 2, nv), vm(3, 2, nv, 2),
                 vm(2, nv), vm(2, 2, nv), vm(2, 2, nv), vm(2, 2, nv),
-                pltpu.SemaphoreType.DMA((4,)),
+                pltpu.SemaphoreType.DMA((5,)),
                 pltpu.SemaphoreType.DMA((5, 2)), pltpu.SemaphoreType.DMA((5, 2)),
                 pltpu.SemaphoreType.DMA((5, 2)), pltpu.SemaphoreType.DMA((5, 2)),
             ],
             compiler_params=pltpu.CompilerParams(collective_id=0, has_side_effects=True),
         )(coupling, face_type, face_rot, flow_state, timestep)
+        return pl.pallas_call(
+            write_out,
+            out_shape=(out, out),
+            in_specs=[vmem, vmem],
+            out_specs=(any_spec, any_spec),
+            scratch_shapes=[pltpu.SemaphoreType.DMA((2,))],
+        )(*(pltpu.with_memory_space_constraint(m, pltpu.VMEM) for m in made))
 
     return jax.shard_map(
         body,

time: 22.7 us -> 19.5 us (0.86)
  local copies, waits for them, and re-layouts: 2.34 us -> 0 us
  Pallas kernels: 19.5 us -> 18.7 us
    unnamed x4 -> x0, local copies, waits for them, and re-layouts: 2.34 us -> none
    pallas_call x1 -> x2, Pallas kernels: 19.5 us -> 18.7 us  [the longest x1 18 us: body(): pl.pallas_call(functools.partial(kernel, nb, ns), out_shape=(held, held),...]
where the time goes in v2:
time: 19.5 us; the launch traced here: 19.4 us
  Pallas kernels  18.7 us (96%)
  between operations  0.64 us (3%)
    pallas_call x1, Pallas kernels, body(): pl.pallas_call(functools.partial(kernel, nb, ns), out_shape=(held, held),...  18 us
    pallas_call x1, Pallas kernels, body(): pl.pallas_call(write_out, out_shape=(out, out), in_specs=[vmem, vmem], ou...  0.76 us

profile of v2, /device:TPU:0, one launch (start us, length us, event | category | flops | bytes accessed | tf_op | source)
XLA Modules:
  0.0 19.4 jit_solution(3619009748230558844)
XLA Ops:
  0.6 18.0 %shard_map.68 = (f32[6,8,8,128]{3,2,1,0:T(8,128)S(1)}, f32[6,8,8,128]{3,2,1,0:T(8,128)S(1)}) custom-call(f32[3,6,6]{2,1,0:T(8,128)} %coup_hbm.1, s32[1,2]{1,0:T(1,128)} %ftype_hbm.1, s32[1,2]{1,0:T(1,128)} %frot_hbm.1, f32[6,8,8,128]{3,2,1,0:T(8,128)} %q_hbm.1, f32[8,8,128]{2,1,0:T(8,128)} %dt_hbm.1), custom_call_target="tpu_custom_call" | custom-call | tf_op jit(solution)/shard_map/pallas_call | solution.py:411
  18.6 0.8 %shard_map.69 = (f32[6,8,8,128]{3,2,1,0:T(8,128)}, f32[6,8,8,128]{3,2,1,0:T(8,128)}) custom-call(f32[6,8,8,128]{3,2,1,0:T(8,128)S(1)} %get-tuple-element.4.upd, f32[6,8,8,128]{3,2,1,0:T(8,128)S(1)} %get-tuple-element.5.res), custom_call_target="tpu_custom_call" | custom-call | tf_op jit(solution)/shard_map/pallas_call | solution.py:430

commit v3 on v2

--- a/solution.py
+++ b/solution.py
@@ -126,16 +126,25 @@
 
         lax.fori_loop(0, n // step, row, 0)
 
+    width = 4 * rows
+    per = nk // width
+
     def pack(ref, dst, n, h):
         group = kk // (4 * h)
         packed = []
-        for v in range(NV):
-            p = roll(ref[v, 2], 2 * h, 1)
-            for i in range(1, n):
-                p = jnp.where(group == i, roll(ref[v, 2 + i], 2 * h + 4 * h * i, 1), p)
-            dst[v] = p
+        for first in range(0, NV, per):
+            p = None
+            for v in range(first, min(first + per, NV)):
+                for i in range(n):
+                    spot = (v - first) * n + i
+                    x = roll(ref[v, 2 + i], 2 * h + 4 * h * spot, 1)
+                    p = x if p is None else jnp.where(group == spot, x, p)
+            dst[first // per] = p
             packed.append(p)
         return packed
+
+    def unpack(packed):
+        return [roll(packed[v // per], -(v % per) * width, 1) for v in range(NV)]
 
     def k_edges(low, high, h):
         r = kk % (4 * h)
@@ -150,9 +159,10 @@
         return out
 
     def k_correction(own, ref, h):
-        low = [jnp.where(jnp.full(shape, sub) > 0, ref[0, v], 0.0) for v in range(NV)]
-        high = [jnp.where(jnp.full(shape, sub) < ns - 1, ref[1, v], 0.0) for v in range(NV)]
-        got = k_edges(low, high, h)
+        count = ref.shape[1]
+        low = [jnp.where(jnp.full(shape, sub) > 0, ref[0, n], 0.0) for n in range(count)]
+        high = [jnp.where(jnp.full(shape, sub) < ns - 1, ref[1, n], 0.0) for n in range(count)]
+        got = k_edges(unpack(low), unpack(high), h)
         return [got[v] - own[v] for v in range(NV)]
 
     def flip(x):
@@ -288,9 +298,10 @@
         load.wait()
     kinds = [splat(ftype, side) for side in (0, 1)]
     rots = [splat(frot, side) for side in (0, 1)]
-    own = k_edges(*[pack(q0, pf_s.at[0], rows, 1)] * 2, 1)
+    packed = pack(q0, pf_s.at[0], rows, 1)
     k0 = sub_copies(0, pf_s.at[0], pf_r.at[0])
     sub_go(k0)
+    own = k_edges(*[unpack(packed)] * 2, 1)
     own_part(q0, acc, rows, 1)
     for i in range(crows):
         cst[i] = 0.125 * pair_sum(dt[2 * i] + dt[2 * i + 1])
@@ -306,9 +317,10 @@
 
     h1 = blk_copies(1, s1.at[:, pl.ds(rows, 2)], s1.at[:, pl.ds(2, 2)], hf_r.at[1])
     go(h1)
-    own = k_edges(*[pack(s1, pf_s.at[1], rows, 1)] * 2, 1)
+    packed = pack(s1, pf_s.at[1], rows, 1)
     k1 = sub_copies(1, pf_s.at[1], pf_r.at[1])
     sub_go(k1)
+    own = k_edges(*[unpack(packed)] * 2, 1)
     own_part(s1, acc, rows, 1)
     sub_got(k1)
     kc = k_correction(own, pf_r.at[1], 1)
@@ -322,18 +334,20 @@
 
     h2 = blk_copies(2, s2.at[:, pl.ds(rows, 2)], s2.at[:, pl.ds(2, 2)], hf_r.at[2])
     go(h2)
-    own = k_edges(*[pack(s2, pf_s.at[2], rows, 1)] * 2, 1)
+    packed = pack(s2, pf_s.at[2], rows, 1)
     k2 = sub_copies(2, pf_s.at[2], pf_r.at[2])
     sub_go(k2)
+    own = k_edges(*[unpack(packed)] * 2, 1)
     for v in range(NV):
         for i in range(crows):
             cs[v, 2 + i] = 0.125 * pair_sum(s2[v, 2 + 2 * i] + s2[v, 3 + 2 * i])
     coarse_rows(0, cs)
     h3 = blk_copies(3, hc_s.at[0, 0], hc_s.at[0, 1], hc_r.at[0])
     go(h3)
-    own_c = k_edges(*[pack(cs, pc_s.at[0], crows, 2)] * 2, 2)
+    packed = pack(cs, pc_s.at[0], crows, 2)
     k3 = sub_copies(3, pc_s.at[0], pc_r.at[0])
     sub_go(k3)
+    own_c = k_edges(*[unpack(packed)] * 2, 2)
     own_part(s2, acc, rows, 1)
     sub_got(k2)
     kc = k_correction(own, pf_r.at[2], 1)
@@ -353,9 +367,10 @@
     coarse_rows(1, c1)
     h4 = blk_copies(4, hc_s.at[1, 0], hc_s.at[1, 1], hc_r.at[1])
     go(h4)
-    own_d = k_edges(*[pack(c1, pc_s.at[1], crows, 2)] * 2, 2)
+    packed = pack(c1, pc_s.at[1], crows, 2)
     k4 = sub_copies(4, pc_s.at[1], pc_r.at[1])
     sub_go(k4)
+    own_d = k_edges(*[unpack(packed)] * 2, 2)
     own_part(cs, cacc, crows, 2)
     sub_got(k3)
     kc = k_correction(own_c, pc_r.at[0], 2)
@@ -403,6 +418,7 @@
         nv, rows, nj, nk = flow_state.shape
         f32 = jnp.float32
         half = rows // 2
+        ends = -(-nv // (nk // (4 * rows)))
         any_spec = pl.BlockSpec(memory_space=pl.ANY)
         vm = lambda *s: pltpu.VMEM(s + (nj, nk), f32)
         out = jax.ShapeDtypeStruct(flow_state.shape, f32)
@@ -419,8 +435,8 @@
                 vm(nv, rows + 4), vm(nv, rows + 4), vm(nv, rows + 4), vm(rows),
                 vm(nv, rows), vm(nv, half), vm(nv, half), vm(nv, half),
                 vm(nv, half + 4), vm(nv, half + 4), vm(half),
-                vm(3, nv), vm(3, 2, nv), vm(3, 2, nv, 2),
-                vm(2, nv), vm(2, 2, nv), vm(2, 2, nv), vm(2, 2, nv),
+                vm(3, ends), vm(3, 2, ends), vm(3, 2, nv, 2),
+                vm(2, ends), vm(2, 2, ends), vm(2, 2, nv), vm(2, 2, nv),
                 pltpu.SemaphoreType.DMA((5,)),
                 pltpu.SemaphoreType.DMA((5, 2)), pltpu.SemaphoreType.DMA((5, 2)),
                 pltpu.SemaphoreType.DMA((5, 2)), pltpu.SemaphoreType.DMA((5, 2)),

time: 19.5 us -> 19.1 us (0.979)
  Pallas kernels: 18.7 us -> 18.4 us
    pallas_call x1, Pallas kernels: 18 us -> 17.6 us  [body(): pl.pallas_call(functools.partial(kernel, nb, ns), out_shape=(held, held),...]
where the time goes in v3:
time: 19.1 us; the launch traced here: 19 us
  Pallas kernels  18.4 us (96%)
  between operations  0.64 us (3%)
    pallas_call x1, Pallas kernels, body(): pl.pallas_call(functools.partial(kernel, nb, ns), out_shape=(held, held),...  17.6 us
    pallas_call x1, Pallas kernels, body(): pl.pallas_call(write_out, out_shape=(out, out), in_specs=[vmem, vmem], ou...  0.76 us

profile of v3, /device:TPU:0, one launch (start us, length us, event | category | flops | bytes accessed | tf_op | source)
XLA Modules:
  0.0 19.0 jit_solution(17623445397957085712)
XLA Ops:
  0.6 17.6 %shard_map.68 = (f32[6,8,8,128]{3,2,1,0:T(8,128)S(1)}, f32[6,8,8,128]{3,2,1,0:T(8,128)S(1)}) custom-call(f32[3,6,6]{2,1,0:T(8,128)} %coup_hbm.1, s32[1,2]{1,0:T(1,128)} %ftype_hbm.1, s32[1,2]{1,0:T(1,128)} %frot_hbm.1, f32[6,8,8,128]{3,2,1,0:T(8,128)} %q_hbm.1, f32[8,8,128]{2,1,0:T(8,128)} %dt_hbm.1), custom_call_target="tpu_custom_call" | custom-call | tf_op jit(solution)/shard_map/pallas_call | solution.py:427
  18.2 0.8 %shard_map.69 = (f32[6,8,8,128]{3,2,1,0:T(8,128)}, f32[6,8,8,128]{3,2,1,0:T(8,128)}) custom-call(f32[6,8,8,128]{3,2,1,0:T(8,128)S(1)} %get-tuple-element.4.upd, f32[6,8,8,128]{3,2,1,0:T(8,128)S(1)} %get-tuple-element.5.res), custom_call_target="tpu_custom_call" | custom-call | tf_op jit(solution)/shard_map/pallas_call | solution.py:446

commit v4 on v3

--- a/solution.py
+++ b/solution.py
@@ -313,10 +313,12 @@
     def store1(v, i, r):
         s1[v, 2 + i] = q0[v, 2 + i] - FIRST * dt[i] * r
 
-    finish(acc, rows, 1, kc, i_edges(before, after, q0, rows), store1, edge_first)
-
+    edges = i_edges(before, after, q0, rows)
+    finish(acc, rows, 1, kc, edges, store1, edge_first[:4])
     h1 = blk_copies(1, s1.at[:, pl.ds(rows, 2)], s1.at[:, pl.ds(2, 2)], hf_r.at[1])
     go(h1)
+    finish(acc, rows, 1, kc, edges, store1, edge_first[4:])
+
     packed = pack(s1, pf_s.at[1], rows, 1)
     k1 = sub_copies(1, pf_s.at[1], pf_r.at[1])
     sub_go(k1)
@@ -330,10 +332,12 @@
     def store2(v, i, r):
         s2[v, 2 + i] = q0[v, 2 + i] - dt[i] * r
 
-    finish(acc, rows, 1, kc, i_edges(before, after, s1, rows), store2, edge_first)
-
+    edges = i_edges(before, after, s1, rows)
+    finish(acc, rows, 1, kc, edges, store2, edge_first[:4])
     h2 = blk_copies(2, s2.at[:, pl.ds(rows, 2)], s2.at[:, pl.ds(2, 2)], hf_r.at[2])
     go(h2)
+    finish(acc, rows, 1, kc, edges, store2, edge_first[4:])
+
     packed = pack(s2, pf_s.at[2], rows, 1)
     k2 = sub_copies(2, pf_s.at[2], pf_r.at[2])
     sub_go(k2)

time: 19.1 us -> 19.1 us (level)
  no operation moved by 1% of the time
where the time goes in v4:
time: 19.1 us; the launch traced here: 19 us
  Pallas kernels  18.3 us (96%)
  between operations  0.64 us (3%)
    pallas_call x1, Pallas kernels, body(): pl.pallas_call(functools.partial(kernel, nb, ns), out_shape=(held, held),...  17.6 us
    pallas_call x1, Pallas kernels, body(): pl.pallas_call(write_out, out_shape=(out, out), in_specs=[vmem, vmem], ou...  0.76 us

profile of v4, /device:TPU:0, one launch (start us, length us, event | category | flops | bytes accessed | tf_op | source)
XLA Modules:
  0.0 19.0 jit_solution(1123589324734606283)
XLA Ops:
  0.6 17.6 %shard_map.68 = (f32[6,8,8,128]{3,2,1,0:T(8,128)S(1)}, f32[6,8,8,128]{3,2,1,0:T(8,128)S(1)}) custom-call(f32[3,6,6]{2,1,0:T(8,128)} %coup_hbm.1, s32[1,2]{1,0:T(1,128)} %ftype_hbm.1, s32[1,2]{1,0:T(1,128)} %frot_hbm.1, f32[6,8,8,128]{3,2,1,0:T(8,128)} %q_hbm.1, f32[8,8,128]{2,1,0:T(8,128)} %dt_hbm.1), custom_call_target="tpu_custom_call" | custom-call | tf_op jit(solution)/shard_map/pallas_call | solution.py:431
  18.2 0.8 %shard_map.69 = (f32[6,8,8,128]{3,2,1,0:T(8,128)}, f32[6,8,8,128]{3,2,1,0:T(8,128)}) custom-call(f32[6,8,8,128]{3,2,1,0:T(8,128)S(1)} %get-tuple-element.4.upd, f32[6,8,8,128]{3,2,1,0:T(8,128)S(1)} %get-tuple-element.5.res), custom_call_target="tpu_custom_call" | custom-call | tf_op jit(solution)/shard_map/pallas_call | solution.py:450
